TPU v7x, 32 devices: a whole 2x2x4 slice. The times are simulated.
32 devices in a mesh: fsdp: 2 (over x), ctx: 4 (over y, core), tp: 4 (over z).
Axes of the slice: x: 2, y: 2, z: 4, core: 2. Of those that a mesh axis runs over, the one named last changes fastest.
Arguments:
- tokens: bfloat16 [8, 1024, 2048], P('fsdp', 'ctx'), may hold values from -8 to 8
- positions: int32 [8, 1024], P('fsdp', 'ctx'), may hold values from 0 to 383, as said below
- block_ids: int32 [8, 1024], P('fsdp', 'ctx'), may hold values from 0 to 3, as said below
- gain_attend: bfloat16 [2048], P('fsdp'), may hold values from 0.099609375 to 1.8984375
- w_query: bfloat16 [2048, 2048], P('fsdp', 'tp'), may hold values from -0.125 to 0.125
- w_key: bfloat16 [2048, 2048], P('fsdp', 'tp'), may hold values from -0.125 to 0.125
- w_value: bfloat16 [2048, 2048], P('fsdp', 'tp'), may hold values from -0.125 to 0.125
- w_output: bfloat16 [2048, 2048], P('tp', 'fsdp'), may hold values from -1 to 1
- gain_feed: bfloat16 [2048], P('fsdp'), may hold values from 0.099609375 to 1.8984375
- w_gate: bfloat16 [2048, 8192], P('fsdp', 'tp'), may hold values from -0.125 to 0.125
- w_up: bfloat16 [2048, 8192], P('fsdp', 'tp'), may hold values from -0.125 to 0.125
- w_down: bfloat16 [8192, 2048], P('tp', 'fsdp'), may hold values from -0.0625 to 0.0625
- cotangent: bfloat16 [8, 1024, 2048], P('fsdp', 'ctx'), may hold values from -6 to 6
Outputs:
- layer_out: bfloat16 [8, 1024, 2048], P('fsdp', 'ctx')
- grad_input: bfloat16 [8, 1024, 2048], P('fsdp', 'ctx')
- grad_gain_attend: float32 [2048], P(('fsdp', 'ctx'))
- grad_w_query: float32 [2048, 2048], P(('fsdp', 'ctx'), 'tp')
- grad_w_key: float32 [2048, 2048], P(('fsdp', 'ctx'), 'tp')
- grad_w_value: float32 [2048, 2048], P(('fsdp', 'ctx'), 'tp')
- grad_w_output: float32 [2048, 2048], P('tp', ('fsdp', 'ctx'))
- grad_gain_feed: float32 [2048], P(('fsdp', 'ctx'))
- grad_w_gate: float32 [2048, 8192], P(('fsdp', 'ctx'), 'tp')
- grad_w_up: float32 [2048, 8192], P(('fsdp', 'ctx'), 'tp')
- grad_w_down: float32 [8192, 2048], P('tp', ('fsdp', 'ctx'))
- stream_rms: float32 [], replicated
- attend_rms: float32 [], replicated
- feed_rms: float32 [], replicated
Inputs may be any that keep to these rules, and one draw needn't show every extreme that they name: Along each sequence, positions count 0, 1, 2 and so on from the first token of each block, a run of equal block ids. `block_ids`: along each sequence block ids start at 0, never fall and rise by one at each new block.
All inputs are finite; a program needn't handle non-finite values.
Results may differ from a plain program's by a relative error of at most 0.015.
Values may be sent and summed in bfloat16 or wider, within the bound.
A program may use at most 256 MiB of HBM per device.

v0:
```python
import math
import jax
import jax.numpy as jnp
from jax import lax
from jax.sharding import PartitionSpec as P

HD = 128
norm_epsilon = 1e-05
rope_base = 10000.0


def plain_dot(left_side, right_side):
    return jnp.dot(left_side, right_side, preferred_element_type=jnp.float32)


def dot_last(left_side, right_side):
    return lax.dot_general(
        left_side, right_side, (((1,), (1,)), ((), ())), preferred_element_type=jnp.float32
    )


def dot_first(left_side, right_side):
    return lax.dot_general(
        left_side, right_side, (((0,), (0,)), ((), ())), preferred_element_type=jnp.float32
    )


def inverse_rms(values):
    return lax.rsqrt(jnp.mean(values * values, axis=-1, keepdims=True) + norm_epsilon)


def norm_back(grad_norm, values, scale_rows, gain):
    weighted = grad_norm * gain
    inner_mean = jnp.mean(weighted * values, axis=-1, keepdims=True)
    grad_values = (
        scale_rows * weighted - values * (scale_rows * scale_rows * scale_rows) * inner_mean
    )
    grad_gain = jnp.sum(grad_norm * (values * scale_rows), axis=0)
    return (grad_values, grad_gain)


def rope_tables(positions, head_size):
    half_size = head_size // 2
    inverse = jnp.exp(
        jnp.arange(half_size, dtype=jnp.float32) * (-2.0 * math.log(rope_base) / head_size)
    )
    turned = positions.astype(jnp.float32)[..., None, None] * inverse
    return (jnp.cos(turned), jnp.sin(turned))


def rotate(values, cosine, sine_table, direction):
    half_size = values.shape[-1] // 2
    first_half = values[..., :half_size]
    second_half = values[..., half_size:]
    return jnp.concatenate(
        [
            first_half * cosine - direction * (second_half * sine_table),
            direction * (first_half * sine_table) + second_half * cosine,
        ],
        axis=-1,
    )


def local(
    tokens,
    positions,
    block_ids,
    gain_attend,
    w_query,
    w_key,
    w_value,
    w_output,
    gain_feed,
    w_gate,
    w_up,
    w_down,
    cotangent,
):
    seq_count, block_len, model_width = tokens.shape
    row_count = seq_count * block_len
    seq_len = block_len * lax.axis_size("ctx")
    heads_here = w_query.shape[1] // HD
    score_scale = 1.0 / math.sqrt(HD)
    score_shift = math.log(seq_len)
    shape_heads = (seq_count, block_len, heads_here, HD)
    stream = tokens.reshape(row_count, model_width).astype(jnp.float32)
    query_full, key_full, value_full, output_full, gain_one = (
        lax.all_gather(w_query, "fsdp", axis=0, tiled=True),
        lax.all_gather(w_key, "fsdp", axis=0, tiled=True),
        lax.all_gather(w_value, "fsdp", axis=0, tiled=True),
        lax.all_gather(w_output, "fsdp", axis=1, tiled=True),
        lax.all_gather(gain_attend, "fsdp", axis=0, tiled=True),
    )
    gain_one = gain_one.astype(jnp.float32)
    scale_one = inverse_rms(stream)
    normed_one = (stream * scale_one * gain_one).astype(jnp.bfloat16)
    queries = plain_dot(normed_one, query_full)
    key_proj = plain_dot(normed_one, key_full)
    values = plain_dot(normed_one, value_full).astype(jnp.bfloat16)
    cosine, sine_table = rope_tables(positions, HD)
    query_rot = rotate(queries.reshape(shape_heads), cosine, sine_table, 1.0).astype(jnp.bfloat16)
    key_rot = (
        rotate(key_proj.reshape(shape_heads), cosine, sine_table, 1.0)
        .astype(jnp.bfloat16)
        .reshape(seq_count, block_len, heads_here * HD)
    )
    value_rows = values.reshape(seq_count, block_len, heads_here * HD)
    query_tags = block_ids.astype(jnp.float32)
    key_tags = block_ids.astype(jnp.bfloat16)

    def scores_of(portion):
        key_piece, value_piece, tag_piece = portion
        span = key_piece.shape[1]
        key_heads = key_piece.reshape(seq_count, span, heads_here, HD)
        value_heads = value_piece.reshape(seq_count, span, heads_here, HD)
        logits = (
            jnp.einsum("sqhd,skhd->shqk", query_rot, key_heads, preferred_element_type=jnp.float32)
            * score_scale
            - score_shift
        )
        allowed = tag_piece.astype(jnp.float32)[:, None, None, :] <= query_tags[:, None, :, None]
        return (key_heads, value_heads, jax.nn.sigmoid(logits), allowed)

    key_heads, value_heads, squashed, allowed = scores_of(
        (
            lax.all_gather(key_rot, "ctx", axis=1, tiled=True),
            lax.all_gather(value_rows, "ctx", axis=1, tiled=True),
            lax.all_gather(key_tags, "ctx", axis=1, tiled=True),
        )
    )
    weights = jnp.where(allowed, squashed, 0.0).astype(jnp.bfloat16)
    attended = jnp.einsum(
        "shqk,skhd->sqhd", weights, value_heads, preferred_element_type=jnp.float32
    )
    mixed_rows = attended.reshape(row_count, heads_here * HD).astype(jnp.bfloat16)
    attend_out = lax.psum(plain_dot(mixed_rows, output_full), "tp")
    middle = stream + attend_out
    gate_full, up_full, down_full, gain_two = (
        lax.all_gather(w_gate, "fsdp", axis=0, tiled=True),
        lax.all_gather(w_up, "fsdp", axis=0, tiled=True),
        lax.all_gather(w_down, "fsdp", axis=1, tiled=True),
        lax.all_gather(gain_feed, "fsdp", axis=0, tiled=True),
    )
    gain_two = gain_two.astype(jnp.float32)
    scale_two = inverse_rms(middle)
    normed_two = (middle * scale_two * gain_two).astype(jnp.bfloat16)
    gate_vals = plain_dot(normed_two, gate_full)
    up_vals = plain_dot(normed_two, up_full)
    gate_sig = jax.nn.sigmoid(gate_vals)
    gate_act = gate_vals * gate_sig
    hidden = (gate_act * up_vals).astype(jnp.bfloat16)
    feed_out = lax.psum(plain_dot(hidden, down_full), "tp")
    result = middle + feed_out
    layer_out = result.astype(jnp.bfloat16).reshape(tokens.shape)
    totals = lax.psum(
        (jnp.sum(result * result), jnp.sum(attend_out * attend_out), jnp.sum(feed_out * feed_out)),
        ("fsdp", "ctx"),
    )
    entries = float(row_count * model_width * lax.axis_size("fsdp") * lax.axis_size("ctx"))
    stream_rms = jnp.sqrt(totals[0] / entries)
    attend_rms = jnp.sqrt(totals[1] / entries)
    feed_rms = jnp.sqrt(totals[2] / entries)
    query_full, key_full, value_full, output_full, gate_full, up_full, down_full = (
        lax.all_gather(w_query, "fsdp", axis=0, tiled=True),
        lax.all_gather(w_key, "fsdp", axis=0, tiled=True),
        lax.all_gather(w_value, "fsdp", axis=0, tiled=True),
        lax.all_gather(w_output, "fsdp", axis=1, tiled=True),
        lax.all_gather(w_gate, "fsdp", axis=0, tiled=True),
        lax.all_gather(w_up, "fsdp", axis=0, tiled=True),
        lax.all_gather(w_down, "fsdp", axis=1, tiled=True),
    )
    grad_rows = cotangent.reshape(row_count, model_width)
    grad_stream = grad_rows.astype(jnp.float32)
    grad_hidden = dot_last(grad_rows, down_full)
    grad_down = dot_first(hidden, grad_rows)
    slope = gate_sig * (1.0 + gate_vals * (1.0 - gate_sig))
    grad_gate = (grad_hidden * up_vals * slope).astype(jnp.bfloat16)
    grad_up = (grad_hidden * gate_act).astype(jnp.bfloat16)
    grad_normed_two = lax.psum(dot_last(grad_gate, gate_full) + dot_last(grad_up, up_full), "tp")
    grad_gate_w = dot_first(normed_two, grad_gate)
    grad_up_w = dot_first(normed_two, grad_up)
    grad_middle_norm, grad_gain_two = norm_back(grad_normed_two, middle, scale_two, gain_two)
    grad_middle = grad_stream + grad_middle_norm
    grad_attend = grad_middle.astype(jnp.bfloat16)
    grad_mixed = dot_last(grad_attend, output_full).astype(jnp.bfloat16)
    grad_output_w = dot_first(mixed_rows, grad_attend)
    grad_mixed_heads = grad_mixed.reshape(shape_heads)
    key_heads, value_heads, squashed, allowed = scores_of(
        (
            lax.all_gather(key_rot, "ctx", axis=1, tiled=True),
            lax.all_gather(value_rows, "ctx", axis=1, tiled=True),
            lax.all_gather(key_tags, "ctx", axis=1, tiled=True),
        )
    )
    span = key_heads.shape[1]
    weights = jnp.where(allowed, squashed, 0.0).astype(jnp.bfloat16)
    grad_weights = jnp.einsum(
        "sqhd,skhd->shqk", grad_mixed_heads, value_heads, preferred_element_type=jnp.float32
    )
    grad_logits = jnp.where(allowed, grad_weights * squashed * (1.0 - squashed), 0.0).astype(
        jnp.bfloat16
    )
    grad_query = score_scale * jnp.einsum(
        "shqk,skhd->sqhd", grad_logits, key_heads, preferred_element_type=jnp.float32
    )
    key_part = (
        score_scale
        * jnp.einsum("shqk,sqhd->skhd", grad_logits, query_rot, preferred_element_type=jnp.float32)
    ).reshape(seq_count, span, heads_here * HD)
    value_part = jnp.einsum(
        "shqk,sqhd->skhd", weights, grad_mixed_heads, preferred_element_type=jnp.float32
    ).reshape(seq_count, span, heads_here * HD)
    grad_key_mine, grad_value_mine = (
        lax.psum_scatter(key_part, "ctx", scatter_dimension=1, tiled=True),
        lax.psum_scatter(value_part, "ctx", scatter_dimension=1, tiled=True),
    )
    grad_query_rows = (
        rotate(grad_query, cosine, sine_table, -1.0)
        .reshape(row_count, heads_here * HD)
        .astype(jnp.bfloat16)
    )
    grad_key_rows = (
        rotate(grad_key_mine.reshape(shape_heads), cosine, sine_table, -1.0)
        .reshape(row_count, heads_here * HD)
        .astype(jnp.bfloat16)
    )
    grad_value_rows = grad_value_mine.reshape(row_count, heads_here * HD).astype(jnp.bfloat16)
    grad_normed_one = lax.psum(
        dot_last(grad_query_rows, query_full)
        + dot_last(grad_key_rows, key_full)
        + dot_last(grad_value_rows, value_full),
        "tp",
    )
    grad_query_w = dot_first(normed_one, grad_query_rows)
    grad_key_w = dot_first(normed_one, grad_key_rows)
    grad_value_w = dot_first(normed_one, grad_value_rows)
    grad_input_norm, grad_gain_one = norm_back(grad_normed_one, stream, scale_one, gain_one)
    grad_input = (grad_middle + grad_input_norm).astype(jnp.bfloat16).reshape(tokens.shape)
    summed = (
        lax.psum_scatter(grad_gain_one, ("fsdp", "ctx"), scatter_dimension=0, tiled=True),
        lax.psum_scatter(grad_query_w, ("fsdp", "ctx"), scatter_dimension=0, tiled=True),
        lax.psum_scatter(grad_key_w, ("fsdp", "ctx"), scatter_dimension=0, tiled=True),
        lax.psum_scatter(grad_value_w, ("fsdp", "ctx"), scatter_dimension=0, tiled=True),
        lax.psum_scatter(grad_output_w, ("fsdp", "ctx"), scatter_dimension=1, tiled=True),
        lax.psum_scatter(grad_gain_two, ("fsdp", "ctx"), scatter_dimension=0, tiled=True),
        lax.psum_scatter(grad_gate_w, ("fsdp", "ctx"), scatter_dimension=0, tiled=True),
        lax.psum_scatter(grad_up_w, ("fsdp", "ctx"), scatter_dimension=0, tiled=True),
        lax.psum_scatter(grad_down, ("fsdp", "ctx"), scatter_dimension=1, tiled=True),
    )
    return (
        layer_out,
        grad_input,
        summed[0],
        summed[1],
        summed[2],
        summed[3],
        summed[4],
        summed[5],
        summed[6],
        summed[7],
        summed[8],
        stream_rms,
        attend_rms,
        feed_rms,
    )


def solution(mesh):
    placed = (
        P("fsdp", "ctx", None),
        P("fsdp", "ctx"),
        P("fsdp", "ctx"),
        P("fsdp"),
        P("fsdp", "tp"),
        P("fsdp", "tp"),
        P("fsdp", "tp"),
        P("tp", "fsdp"),
        P("fsdp"),
        P("fsdp", "tp"),
        P("fsdp", "tp"),
        P("tp", "fsdp"),
        P("fsdp", "ctx", None),
    )
    return jax.shard_map(
        local,
        mesh=mesh,
        in_specs=placed,
        out_specs=(
            P("fsdp", "ctx", None),
            P("fsdp", "ctx", None),
            P(("fsdp", "ctx")),
            P(("fsdp", "ctx"), "tp"),
            P(("fsdp", "ctx"), "tp"),
            P(("fsdp", "ctx"), "tp"),
            P("tp", ("fsdp", "ctx")),
            P(("fsdp", "ctx")),
            P(("fsdp", "ctx"), "tp"),
            P(("fsdp", "ctx"), "tp"),
            P("tp", ("fsdp", "ctx")),
            P(),
            P(),
            P(),
        ),
        check_vma=False,
    )
```

profile of v0, /device:TPU:0, one launch (start us, length us, event | category | flops | bytes accessed | tf_op | source)
XLA Modules:
  0.0 2545.2 jit_solution(7070096330234557118)
XLA Ops:
  25.4 20.0 all-gather.16.cloned.1.call-done
  48.3 31.7 %all-gather.14.cloned.1.call-done = bf16[2048,512]{1,0:T(8,128)(2,1)} async-done(((bf16[1024,512]{1,0:T(8,128)(2,1)}), bf16[2048,512]{1,0:T(8,128)(2,1)}) %all-gather.14.cloned.1.call-update) | async-done | bytes 2097168 | tf_op jit(solution)/shard_map/all_gather | solution.py:88
  98.3 16.4 all-gather.10.cloned.1.call-done
  127.6 24.1 all-gather.18.cloned.1.call-done
  151.7 11.6 add_divide_fusion
  163.3 24.9 all-gather.12.cloned.1.call-done
  188.2 6.2 copy.50
  194.4 11.0 fusion.27
  206.1 16.6 all-gather.20.cloned.1.call-done
  222.7 7.2 fusion.37
  236.9 284.1 %all-reduce.8.cloned.1.call-done = f32[1024,2048]{1,0:T(8,128)} async-done(((f32[1024,2048]{1,0:T(8,128)}), f32[1024,2048]{1,0:T(8,128)}) %all-reduce.8.cloned.1.call-update) | async-done | bytes 8388624 | tf_op jit(solution)/shard_map/psum | solution.py:136
  520.9 7.6 multiply_reduce_fusion.5
  535.6 89.9 %all-gather.22.cloned.1.call-done = bf16[2048,2048]{1,0:T(8,128)(2,1)} async-done(((bf16[1024,2048]{1,0:T(8,128)(2,1)}), bf16[2048,2048]{1,0:T(8,128)(2,1)}) %all-gather.22.cloned.1.call-update) | async-done | bytes 8388624 | tf_op jit(solution)/shard_map/all_gather | solution.py:139
  625.5 14.6 fusion.51
  640.0 91.0 %all-gather.24.cloned.1.call-done = bf16[2048,2048]{1,0:T(8,128)(2,1)} async-done(((bf16[1024,2048]{1,0:T(8,128)(2,1)}), bf16[2048,2048]{1,0:T(8,128)(2,1)}) %all-gather.24.cloned.1.call-update) | async-done | bytes 8388624 | tf_op jit(solution)/shard_map/all_gather | solution.py:140
  731.0 14.5 fusion.52
  745.5 90.9 %all-gather.26.cloned.1.call-done = bf16[2048,2048]{1,0:T(8,128)(2,1)} async-done(((bf16[2048,1024]{1,0:T(8,128)(2,1)}), bf16[2048,2048]{1,0:T(8,128)(2,1)}) %all-gather.26.cloned.1.call-update) | async-done | bytes 8388624 | tf_op jit(solution)/shard_map/all_gather | solution.py:141
  836.4 21.9 multiply_convert_fusion
  858.3 12.7 fusion.54
  871.1 12.7 fusion.53
  883.8 13.3 convolution_add_fusion
  897.2 562.3 %all-reduce.12.cloned.1.call-done = (f32[1024,2048]{1,0:T(8,128)}, f32[1024,2048]{1,0:T(8,128)}) async-done(((f32[1024,2048]{1,0:T(8,128)}, f32[1024,2048]{1,0:T(8,128)}), (f32[1024,2048]{1,0:T(8,128)}, f32[1024,2048]{1,0:T(8,128)})) %all-reduce.12.cloned.1.call-update) | async-done | bytes 16777232 | tf_op jit(solution)/shard_map/psum | solution.py:152
  1459.6 15.1 multiply_reduce_fusion
  1489.3 9.5 select_convert_fusion
  1498.8 6.3 broadcast_multiply_fusion
  1505.2 13.1 fusion.17
  1518.3 9.0 copy.61
  1527.4 7.7 multiply_bitcast_fusion
  1535.1 40.4 %reduce-scatter.10.cloned.1.call-done = f32[4,256,512]{1,2,0:T(8,128)} async-done(((f32[4,1024,512]{1,2,0:T(8,128)}), f32[4,256,512]{1,2,0:T(8,128)}) %reduce-scatter.10.cloned.1.call-update) | async-done | bytes 2097168 | tf_op jit(solution)/shard_map/reduce_scatter | solution.py:214
  1580.6 68.9 %reduce-scatter.12.cloned.1.call-done = f32[4,256,512]{2,1,0:T(8,128)} async-done(((f32[4,1024,512]{2,1,0:T(8,128)}), f32[4,256,512]{2,1,0:T(8,128)}) %reduce-scatter.12.cloned.1.call-update) | async-done | bytes 2097168 | tf_op jit(solution)/shard_map/reduce_scatter | solution.py:215
  1665.1 7.7 fusion.19
  1672.9 15.6 fusion.55
  1688.5 15.4 fusion.56
  1704.0 15.6 fusion.57
  1719.7 6.6 convolution_bitcast_fusion
  1726.4 6.6 fusion.32
  1733.1 6.5 fusion.28
  1741.0 213.9 %all-reduce.10.cloned.1.call-done = f32[1024,2048]{1,0:T(8,128)} async-done(((f32[1024,2048]{1,0:T(8,128)}), f32[1024,2048]{1,0:T(8,128)}) %all-reduce.10.cloned.1.call-update) | async-done | bytes 8388624 | tf_op jit(solution)/shard_map/psum | solution.py:228
  1954.9 6.4 fusion.3
  1961.3 25.5 %all-reduce.2 = (f32[2048]{0:T(1024)S(1)}, f32[2048]{0:T(1024)S(1)}, f32[]{:T(128)}, f32[]{:T(128)}, f32[]{:T(128)}) all-reduce(f32[2048]{0:T(1024)S(1)} %get-tuple-element.16, f32[2048]{0:T(1024)S(1)} %copy-done.27, f32[]{:T(128)} %get-tuple-element.19, ...), channel_id=4, replica_groups=mesh['fsdp'=2,'ctx'=4,'tp'=4] {'fsdp','ctx'}, use_global_device_ids=true, to_apply=%region_11.12.clone | all-reduce | flops 4099 | bytes 32792
  1990.2 10.5 fusion.10
  2000.6 8.1 reduce-scatter.20.cloned.1.call-done
  2008.8 120.2 %reduce-scatter.22.cloned.1.call-done = f32[256,2048]{1,0:T(8,128)} async-done(((f32[2048,2048]{1,0:T(8,128)}), f32[256,2048]{1,0:T(8,128)}) %reduce-scatter.22.cloned.1.call-update) | async-done | bytes 2097168 | tf_op jit(solution)/shard_map/reduce_scatter | solution.py:246
  2129.0 120.2 %reduce-scatter.24.cloned.1.call-done = f32[256,2048]{1,0:T(8,128)} async-done(((f32[2048,2048]{1,0:T(8,128)}), f32[256,2048]{1,0:T(8,128)}) %reduce-scatter.24.cloned.1.call-update) | async-done | bytes 2097168 | tf_op jit(solution)/shard_map/reduce_scatter | solution.py:247
  2249.2 120.0 %reduce-scatter.26.cloned.1.call-done = f32[2048,256]{1,0:T(8,128)} async-done(((f32[2048,2048]{1,0:T(8,128)}), f32[2048,256]{1,0:T(8,128)}) %reduce-scatter.26.cloned.1.call-update) | async-done | bytes 2097168 | tf_op jit(solution)/shard_map/reduce_scatter | solution.py:248
  2369.2 55.1 %reduce-scatter.18.cloned.1.call-done = f32[256,512]{1,0:T(8,128)} async-done(((f32[2048,512]{1,0:T(8,128)}), f32[256,512]{1,0:T(8,128)}) %reduce-scatter.18.cloned.1.call-update) | async-done | bytes 524304 | tf_op jit(solution)/shard_map/reduce_scatter | solution.py:243
  2424.3 55.0 %reduce-scatter.14.cloned.1.call-done = f32[256,512]{1,0:T(8,128)} async-done(((f32[2048,512]{1,0:T(8,128)}), f32[256,512]{1,0:T(8,128)}) %reduce-scatter.14.cloned.1.call-update) | async-done | bytes 524304 | tf_op jit(solution)/shard_map/reduce_scatter | solution.py:241
  2479.3 55.1 %reduce-scatter.16.cloned.1.call-done = f32[256,512]{1,0:T(8,128)} async-done(((f32[2048,512]{1,0:T(8,128)}), f32[256,512]{1,0:T(8,128)}) %reduce-scatter.16.cloned.1.call-update) | async-done | bytes 524304 | tf_op jit(solution)/shard_map/reduce_scatter | solution.py:242
  (152 shorter events, 104.4 us)
Async XLA Ops:
  7.2 38.2 %all-gather.16.cloned.1.call-start = ((), (), s32[]{:S(2)}) async-start(), calls=%async_computation.12 | async-start | bytes 3145728 | tf_op jit(solution)/shard_map/all_gather | solution.py:89
  7.9 72.1 %all-gather.14.cloned.1.call-start = ((), (), s32[]{:S(2)}) async-start(), calls=%async_computation.11 | async-start | bytes 3145728 | tf_op jit(solution)/shard_map/all_gather | solution.py:88
  8.7 106.1 %all-gather.10.cloned.1.call-start = ((), (), s32[]{:S(2)}) async-start(), calls=%async_computation.9 | async-start | bytes 3145728 | tf_op jit(solution)/shard_map/all_gather | solution.py:90
  9.4 142.3 %all-gather.18.cloned.1.call-start = ((), (), s32[]{:S(2)}) async-start(), calls=%async_computation.13 | async-start | bytes 5242880 | tf_op jit(solution)/shard_map/all_gather | solution.py:126
  14.9 78.2 %copy-start.23 = (f32[2048]{0:T(1024)}, f32[2048]{0:T(1024)S(1)}, u32[]{:S(2)}) copy-start(f32[2048]{0:T(1024)S(1)} %convert_element_type.133) | copy-start | bytes 24580
  25.4 65.7 %copy-start.10 = (f32[4,256,64]{1,2,0:T(8,128)}, f32[4,256,64]{1,2,0:T(8,128)S(1)}, u32[]{:S(2)}) copy-start(f32[4,256,64]{1,2,0:T(8,128)S(1)} %get-tuple-element.48) | copy-start | bytes 786436
  25.4 65.7 %copy-start.12 = (f32[4,256,64]{1,2,0:T(8,128)}, f32[4,256,64]{1,2,0:T(8,128)S(1)}, u32[]{:S(2)}) copy-start(f32[4,256,64]{1,2,0:T(8,128)S(1)} %get-tuple-element.49) | copy-start | bytes 786436
  84.0 4.7 copy-start.16
  91.8 59.9 %copy-start.17 = (bf16[4,256,4,64]{1,3,2,0:T(8,128)(2,1)}, bf16[4,256,4,64]{1,3,2,0:T(8,128)(2,1)S(1)}, u32[]{:S(2)}) copy-start(bf16[4,256,4,64]{1,3,2,0:T(8,128)(2,1)S(1)} %get-tuple-element.40) | copy-start | bytes 1572868
  91.8 59.9 %copy-start.19 = (bf16[4,256,4,64]{1,3,2,0:T(8,128)(2,1)}, bf16[4,256,4,64]{1,3,2,0:T(8,128)(2,1)S(1)}, u32[]{:S(2)}) copy-start(bf16[4,256,4,64]{1,3,2,0:T(8,128)(2,1)S(1)} %get-tuple-element.41) | copy-start | bytes 1572868
  93.0 95.2 %all-gather.12.cloned.1.call-start = ((), (), s32[]{:S(2)}) async-start(), calls=%async_computation.10 | async-start | bytes 5242880 | tf_op jit(solution)/shard_map/all_gather | solution.py:127
  93.1 27.8 %copy-start.25 = (f32[1,2,4,128]{3,1,2,0:T(2,128)}, f32[1,2,4,128]{3,1,2,0:T(2,128)S(1)}, u32[]{:S(2)}) copy-start(f32[1,2,4,128]{3,1,2,0:T(2,128)S(1)} %copy.68) | copy-start | bytes 12292
  98.3 23.2 copy-start.28
  120.9 101.8 %all-gather.20.cloned.1.call-start = ((), (), s32[]{:S(2)}) async-start(), calls=%async_computation.14 | async-start | bytes 3145728 | tf_op jit(solution)/shard_map/all_gather | solution.py:91
  121.5 399.4 %all-reduce.8.cloned.1.call-start = ((), (), s32[]{:S(2)}) async-start(), calls=%async_computation.15 | async-start | bytes 16777216 | tf_op jit(solution)/shard_map/psum | solution.py:136
  127.6 66.8 %copy-start.4 = (pred[4,256,1024]{2,1,0:T(8,128)(4,1)}, pred[4,256,1024]{2,1,0:T(8,128)(4,1)S(1)}, u32[]{:S(2)}) copy-start(pred[4,256,1024]{2,1,0:T(8,128)(4,1)S(1)} %broadcast_compare_fusion) | copy-start | bytes 3145732
  206.1 23.8 copy-start.8
  230.0 395.5 %all-gather.22.cloned.1.call-start = ((), (), s32[]{:S(2)}) async-start(), calls=%async_computation.16 | async-start | bytes 12582912 | tf_op jit(solution)/shard_map/all_gather | solution.py:139
  230.7 500.3 %all-gather.24.cloned.1.call-start = ((), (), s32[]{:S(2)}) async-start(), calls=%async_computation.17 | async-start | bytes 12582912 | tf_op jit(solution)/shard_map/all_gather | solution.py:140
  231.5 605.0 %all-gather.26.cloned.1.call-start = ((), (), s32[]{:S(2)}) async-start(), calls=%async_computation.18 | async-start | bytes 12582912 | tf_op jit(solution)/shard_map/all_gather | solution.py:141
  232.0 1227.5 %all-reduce.12.cloned.1.call-start = ((), (), s32[]{:S(2)}) async-start(), calls=%async_computation.29 | async-start | bytes 33554432 | tf_op jit(solution)/shard_map/psum | solution.py:152
  858.3 12.7 copy-start.30
  871.1 12.7 copy-start.32
  897.2 678.3 %reduce-scatter.10.cloned.1.call-start = ((), (), s32[]{:S(2)}) async-start(), calls=%async_computation.19 | async-start | bytes 10485760 | tf_op jit(solution)/shard_map/reduce_scatter | solution.py:214
  1459.5 15.1 copy-start.3
  1459.6 15.1 copy-start.6
  1482.6 6.7 copy-start.5
  1489.3 9.5 copy-start.18
  1498.8 6.3 copy-start.2
  1505.2 144.3 %reduce-scatter.12.cloned.1.call-start = ((), (), s32[]{:S(2)}) async-start(), calls=%async_computation.20 | async-start | bytes 10485760 | tf_op jit(solution)/shard_map/reduce_scatter | solution.py:215
  1527.3 48.2 %copy-start.11 = (f32[4,256,64]{1,2,0:T(8,128)S(1)}, f32[4,256,64]{1,2,0:T(8,128)}, u32[]{:S(2)}) copy-start(f32[4,256,64]{1,2,0:T(8,128)} %copy-done.10) | copy-start | bytes 786436
  1527.3 48.2 %copy-start.13 = (f32[4,256,64]{1,2,0:T(8,128)S(1)}, f32[4,256,64]{1,2,0:T(8,128)}, u32[]{:S(2)}) copy-start(f32[4,256,64]{1,2,0:T(8,128)} %copy-done.12) | copy-start | bytes 786436
  1527.3 427.5 %all-reduce.10.cloned.1.call-start = ((), (), s32[]{:S(2)}) async-start(), calls=%async_computation.21 | async-start | bytes 16777216 | tf_op jit(solution)/shard_map/psum | solution.py:228
  1579.3 76.4 %copy-start.15 = (bf16[2048,512]{1,0:T(8,128)(2,1)S(1)}, bf16[2048,512]{1,0:T(8,128)(2,1)}, u32[]{:S(2)}) copy-start(bf16[2048,512]{1,0:T(8,128)(2,1)} %all-gather.14.cloned.1.call-done) | copy-start | bytes 6291460
  1649.5 6.1 copy-start.21
  1663.9 344.9 %reduce-scatter.20.cloned.1.call-start = ((), (), s32[]{:S(2)}) async-start(), calls=%async_computation.25 | async-start | bytes 4718592 | tf_op jit(solution)/shard_map/reduce_scatter | solution.py:244
  1672.9 456.1 %reduce-scatter.22.cloned.1.call-start = ((), (), s32[]{:S(2)}) async-start(), calls=%async_computation.26 | async-start | bytes 18874368 | tf_op jit(solution)/shard_map/reduce_scatter | solution.py:246
  1688.5 560.7 %reduce-scatter.24.cloned.1.call-start = ((), (), s32[]{:S(2)}) async-start(), calls=%async_computation.27 | async-start | bytes 18874368 | tf_op jit(solution)/shard_map/reduce_scatter | solution.py:247
  1703.9 665.3 %reduce-scatter.26.cloned.1.call-start = ((), (), s32[]{:S(2)}) async-start(), calls=%async_computation.28 | async-start | bytes 18874368 | tf_op jit(solution)/shard_map/reduce_scatter | solution.py:248
  1719.6 6.8 copy-start.22
  1719.6 704.7 %reduce-scatter.18.cloned.1.call-start = ((), (), s32[]{:S(2)}) async-start(), calls=%async_computation.24 | async-start | bytes 4718592 | tf_op jit(solution)/shard_map/reduce_scatter | solution.py:243
  1726.3 753.0 %reduce-scatter.14.cloned.1.call-start = ((), (), s32[]{:S(2)}) async-start(), calls=%async_computation.22 | async-start | bytes 4718592 | tf_op jit(solution)/shard_map/reduce_scatter | solution.py:241
  1726.4 6.7 copy-start.20
  1733.0 6.7 copy-start.31
  1733.1 7.9 copy-start.26
  1733.1 221.8 %copy-start.24 = (f32[2048]{0:T(1024)S(1)}, f32[2048]{0:T(1024)}, u32[]{:S(2)}) copy-start(f32[2048]{0:T(1024)} %copy-done.23) | copy-start | bytes 24580
  1733.1 801.4 %reduce-scatter.16.cloned.1.call-start = ((), (), s32[]{:S(2)}) async-start(), calls=%async_computation.23 | async-start | bytes 4718592 | tf_op jit(solution)/shard_map/reduce_scatter | solution.py:242
  1739.7 221.6 %copy-start.27 = (f32[2048]{0:T(1024)S(1)}, f32[2048]{0:T(1024)}, u32[]{:S(2)}) copy-start(f32[2048]{0:T(1024)} %get-tuple-element.21) | copy-start | bytes 24580
  (6 other events, 18.1 us)
Sparse Core Ops, SparseCore 0:
  9.5 35.8 all-gather.15
  46.9 33.0 all-gather.13
  81.6 33.0 all-gather.9
  116.7 34.9 all-gather.17
  153.7 34.4 all-gather.11
  189.6 33.0 all-gather.19
  230.1 290.8 all-reduce.7
  522.5 102.9 all-gather.21
  627.0 103.9 all-gather.23
  732.4 103.9 all-gather.25
  897.3 562.2 all-reduce.11
  1505.3 70.1 reduce-scatter.9
  1578.1 71.3 reduce-scatter.11
  1664.0 290.8 all-reduce.9
  1958.6 50.0 reduce-scatter.19
  2012.7 116.1 reduce-scatter.21
  2133.0 116.1 reduce-scatter.23
  2253.2 115.9 reduce-scatter.25
  2373.1 51.1 reduce-scatter.17
  2428.1 51.1 reduce-scatter.13
  2483.3 51.1 reduce-scatter.15
where the time goes:
time: 2550 us
  waiting for transfers between devices  2110 us (83%)
  matrix products  260 us (10%)
  other arithmetic  69.3 us (3%)
  blocking collectives  41.2 us (2%)
  local copies, waits for them, and re-layouts  38.8 us (2%)
    psum x1, waiting for transfers between devices, local(): feed_out = lax.psum(plain_dot(hidden, down_full), 'tp')  562 us
    psum x1, waiting for transfers between devices, local(): attend_out = lax.psum(plain_dot(mixed_rows, output_full), 'tp')  284 us
    psum x1, waiting for transfers between devices, local(): lax.psum(dot_last(grad_query_rows, query_full) + dot_last(grad_key_rows,...  214 us
    reduce_scatter x1, waiting for transfers between devices, local(): lax.psum_scatter(grad_gate_w, ('fsdp', 'ctx'), scatter_dimension=0, tiled...  120 us
    reduce_scatter x1, waiting for transfers between devices, local(): lax.psum_scatter(grad_up_w, ('fsdp', 'ctx'), scatter_dimension=0, tiled=T...  120 us
    reduce_scatter x1, waiting for transfers between devices, local(): lax.psum_scatter(grad_down, ('fsdp', 'ctx'), scatter_dimension=1, tiled=T...  120 us
    all_gather x1, waiting for transfers between devices, local(): lax.all_gather(w_up, 'fsdp', axis=0, tiled=True)  91 us
    all_gather x1, waiting for transfers between devices, local(): lax.all_gather(w_down, 'fsdp', axis=1, tiled=True)  90.9 us
  transfers between devices with their start and end apart: 21, of which 21 were waited for; matrix products, arithmetic and copies ran while one was open for 9% of the time, Pallas kernels for 0%

commit v1 on v0

--- a/solution.py
+++ b/solution.py
@@ -7,6 +7,18 @@
 HD = 128
 norm_epsilon = 1e-05
 rope_base = 10000.0
+
+
+def doubled_up(shard, axis, dim):
+    ways, here = (lax.axis_size(axis), lax.axis_index(axis))
+    grown, reach = (shard, 1)
+    while reach < ways:
+        theirs = lax.ppermute(grown, axis, [(d, d ^ reach) for d in range(ways)])
+        mine_first = jnp.concatenate([grown, theirs], axis=dim)
+        theirs_first = jnp.concatenate([theirs, grown], axis=dim)
+        grown = jnp.where(here & reach == 0, mine_first, theirs_first)
+        reach = 2 * reach
+    return grown
 
 
 def plain_dot(left_side, right_side):
@@ -138,7 +150,7 @@
     gate_full, up_full, down_full, gain_two = (
         lax.all_gather(w_gate, "fsdp", axis=0, tiled=True),
         lax.all_gather(w_up, "fsdp", axis=0, tiled=True),
-        lax.all_gather(w_down, "fsdp", axis=1, tiled=True),
+        doubled_up(w_down, "fsdp", 1),
         lax.all_gather(gain_feed, "fsdp", axis=0, tiled=True),
     )
     gain_two = gain_two.astype(jnp.float32)

time: 2550 us -> 2560 us (level)
  blocking collectives: 41.2 us -> 129 us
  waiting for transfers between devices: 2110 us -> 2030 us
    psum x1, waiting for transfers between devices: 284 us -> 196 us  [local(): attend_out = lax.psum(plain_dot(mixed_rows, output_full), 'tp')]
    all_gather x1, blocking collectives: 4.77 us -> 92.2 us  [local(): lax.all_gather(gain_feed, 'fsdp', axis=0, tiled=True)]
  transfers between devices with their start and end apart: 21 -> 22, of which waited for: 21 -> 21; matrix products, arithmetic and copies ran while one was open for 9% -> 11% of each run, Pallas kernels for 0% -> 0%
where the time goes in v1:
time: 2560 us; the launch traced here: 2550 us
  waiting for transfers between devices  2030 us (79%)
  matrix products  265 us (10%)
  blocking collectives  129 us (5%)
  other arithmetic  69.3 us (3%)
  local copies, waits for them, and re-layouts  38.8 us (2%)
    psum x1, waiting for transfers between devices, local(): feed_out = lax.psum(plain_dot(hidden, down_full), 'tp')  562 us
    psum x1, waiting for transfers between devices, local(): lax.psum(dot_last(grad_query_rows, query_full) + dot_last(grad_key_rows,...  214 us
    psum x1, waiting for transfers between devices, local(): attend_out = lax.psum(plain_dot(mixed_rows, output_full), 'tp')  196 us
    reduce_scatter x1, waiting for transfers between devices, local(): lax.psum_scatter(grad_gate_w, ('fsdp', 'ctx'), scatter_dimension=0, tiled...  120 us
    reduce_scatter x1, waiting for transfers between devices, local(): lax.psum_scatter(grad_up_w, ('fsdp', 'ctx'), scatter_dimension=0, tiled=T...  120 us
    reduce_scatter x1, waiting for transfers between devices, local(): lax.psum_scatter(grad_down, ('fsdp', 'ctx'), scatter_dimension=1, tiled=T...  120 us
    all_gather x1, blocking collectives, local(): lax.all_gather(gain_feed, 'fsdp', axis=0, tiled=True)  92.2 us
    all_gather x1, waiting for transfers between devices, local(): lax.all_gather(w_up, 'fsdp', axis=0, tiled=True)  91.1 us
  transfers between devices with their start and end apart: 22, of which 21 were waited for; matrix products, arithmetic and copies ran while one was open for 11% of the time, Pallas kernels for 0%

profile of v1, /device:TPU:0, one launch (start us, length us, event | category | flops | bytes accessed | tf_op | source)
XLA Modules:
  0.0 2551.0 jit_solution(15852639095356110210)
XLA Ops:
  25.4 20.0 all-gather.16.cloned.1.call-done
  48.3 31.7 %all-gather.14.cloned.1.call-done = bf16[2048,512]{1,0:T(8,128)(2,1)} async-done(((bf16[1024,512]{1,0:T(8,128)(2,1)}), bf16[2048,512]{1,0:T(8,128)(2,1)}) %all-gather.14.cloned.1.call-update) | async-done | bytes 2097168 | tf_op jit(solution)/shard_map/all_gather | solution.py:100
  98.3 16.4 all-gather.10.cloned.1.call-done
  127.6 24.1 all-gather.18.cloned.1.call-done
  151.7 11.6 add_divide_fusion
  163.3 24.9 all-gather.12.cloned.1.call-done
  194.4 11.0 fusion.34
  206.1 16.6 all-gather.20.cloned.1.call-done
  222.7 7.2 fusion.44
  232.5 92.2 %all_gather.53 = bf16[2048]{0:T(1024)(128)(2,1)S(1)} all-gather(bf16[1024]{0:T(1024)(128)(2,1)S(1)} %copy-done.30), channel_id=1, replica_groups=mesh['fsdp'=2,'ctx'=4,'tp'=4] {'fsdp'}, dimensions={0}, use_global_device_ids=true | all-gather | bytes 6144 | tf_op jit(solution)/shard_map/all_gather | solution.py:154
  324.7 196.3 %all-reduce.8.cloned.1.call-done = f32[1024,2048]{1,0:T(8,128)} async-done(((f32[1024,2048]{1,0:T(8,128)}), f32[1024,2048]{1,0:T(8,128)}) %all-reduce.8.cloned.1.call-update) | async-done | bytes 8388624 | tf_op jit(solution)/shard_map/psum | solution.py:148
  520.9 7.6 multiply_reduce_fusion.5
  535.5 89.9 %all-gather.22.cloned.1.call-done = bf16[2048,2048]{1,0:T(8,128)(2,1)} async-done(((bf16[1024,2048]{1,0:T(8,128)(2,1)}), bf16[2048,2048]{1,0:T(8,128)(2,1)}) %all-gather.22.cloned.1.call-update) | async-done | bytes 8388624 | tf_op jit(solution)/shard_map/all_gather | solution.py:151
  625.5 14.4 fusion.59
  639.9 91.1 %all-gather.24.cloned.1.call-done = bf16[2048,2048]{1,0:T(8,128)(2,1)} async-done(((bf16[1024,2048]{1,0:T(8,128)(2,1)}), bf16[2048,2048]{1,0:T(8,128)(2,1)}) %all-gather.24.cloned.1.call-update) | async-done | bytes 8388624 | tf_op jit(solution)/shard_map/all_gather | solution.py:152
  731.0 14.4 fusion.60
  745.5 91.0 %all-gather.26.cloned.1.call-done = bf16[2048,2048]{1,0:T(8,128)(2,1)} async-done(((bf16[2048,1024]{1,0:T(8,128)(2,1)}), bf16[2048,2048]{1,0:T(8,128)(2,1)}) %all-gather.26.cloned.1.call-update) | async-done | bytes 8388624 | tf_op jit(solution)/shard_map/all_gather | solution.py:182
  836.4 21.9 multiply_convert_fusion
  858.3 14.6 fusion.61
  873.0 14.9 convolution_add_fusion
  887.8 15.1 fusion
  903.0 562.3 %all-reduce.12.cloned.1.call-done = (f32[1024,2048]{1,0:T(8,128)}, f32[1024,2048]{1,0:T(8,128)}) async-done(((f32[1024,2048]{1,0:T(8,128)}, f32[1024,2048]{1,0:T(8,128)}), (f32[1024,2048]{1,0:T(8,128)}, f32[1024,2048]{1,0:T(8,128)})) %all-reduce.12.cloned.1.call-update) | async-done | bytes 16777232 | tf_op jit(solution)/shard_map/psum | solution.py:164
  1465.3 15.1 multiply_reduce_fusion
  1495.1 9.5 select_convert_fusion
  1504.6 6.3 broadcast_multiply_fusion
  1511.0 13.1 fusion.24
  1524.1 9.0 copy.61
  1533.2 7.7 multiply_bitcast_fusion
  1540.9 40.4 %reduce-scatter.10.cloned.1.call-done = f32[4,256,512]{1,2,0:T(8,128)} async-done(((f32[4,1024,512]{1,2,0:T(8,128)}), f32[4,256,512]{1,2,0:T(8,128)}) %reduce-scatter.10.cloned.1.call-update) | async-done | bytes 2097168 | tf_op jit(solution)/shard_map/reduce_scatter | solution.py:226
  1586.4 68.9 %reduce-scatter.12.cloned.1.call-done = f32[4,256,512]{2,1,0:T(8,128)} async-done(((f32[4,1024,512]{2,1,0:T(8,128)}), f32[4,256,512]{2,1,0:T(8,128)}) %reduce-scatter.12.cloned.1.call-update) | async-done | bytes 2097168 | tf_op jit(solution)/shard_map/reduce_scatter | solution.py:227
  1670.9 7.7 fusion.26
  1678.7 15.4 fusion.62
  1694.2 15.2 fusion.63
  1709.5 15.5 fusion.64
  1725.1 6.6 convolution_bitcast_fusion
  1731.8 6.6 fusion.39
  1738.5 6.5 fusion.35
  1746.3 214.3 %all-reduce.10.cloned.1.call-done = f32[1024,2048]{1,0:T(8,128)} async-done(((f32[1024,2048]{1,0:T(8,128)}), f32[1024,2048]{1,0:T(8,128)}) %all-reduce.10.cloned.1.call-update) | async-done | bytes 8388624 | tf_op jit(solution)/shard_map/psum | solution.py:240
  1960.7 6.4 fusion.9
  1967.1 25.5 %all-reduce.2 = (f32[2048]{0:T(1024)S(1)}, f32[2048]{0:T(1024)S(1)}, f32[]{:T(128)}, f32[]{:T(128)}, f32[]{:T(128)}) all-reduce(f32[2048]{0:T(1024)S(1)} %get-tuple-element.16, f32[2048]{0:T(1024)S(1)} %copy-done.28, f32[]{:T(128)} %get-tuple-element.19, ...), channel_id=4, replica_groups=mesh['fsdp'=2,'ctx'=4,'tp'=4] {'fsdp','ctx'}, use_global_device_ids=true, to_apply=%region_11.12.clone | all-reduce | flops 4099 | bytes 32792
  1996.0 10.5 fusion.16
  2006.5 8.1 reduce-scatter.20.cloned.1.call-done
  2014.6 120.2 %reduce-scatter.22.cloned.1.call-done = f32[256,2048]{1,0:T(8,128)} async-done(((f32[2048,2048]{1,0:T(8,128)}), f32[256,2048]{1,0:T(8,128)}) %reduce-scatter.22.cloned.1.call-update) | async-done | bytes 2097168 | tf_op jit(solution)/shard_map/reduce_scatter | solution.py:258
  2134.8 120.2 %reduce-scatter.24.cloned.1.call-done = f32[256,2048]{1,0:T(8,128)} async-done(((f32[2048,2048]{1,0:T(8,128)}), f32[256,2048]{1,0:T(8,128)}) %reduce-scatter.24.cloned.1.call-update) | async-done | bytes 2097168 | tf_op jit(solution)/shard_map/reduce_scatter | solution.py:259
  2255.0 120.0 %reduce-scatter.26.cloned.1.call-done = f32[2048,256]{1,0:T(8,128)} async-done(((f32[2048,2048]{1,0:T(8,128)}), f32[2048,256]{1,0:T(8,128)}) %reduce-scatter.26.cloned.1.call-update) | async-done | bytes 2097168 | tf_op jit(solution)/shard_map/reduce_scatter | solution.py:260
  2375.0 55.1 %reduce-scatter.18.cloned.1.call-done = f32[256,512]{1,0:T(8,128)} async-done(((f32[2048,512]{1,0:T(8,128)}), f32[256,512]{1,0:T(8,128)}) %reduce-scatter.18.cloned.1.call-update) | async-done | bytes 524304 | tf_op jit(solution)/shard_map/reduce_scatter | solution.py:255
  2430.1 55.0 %reduce-scatter.14.cloned.1.call-done = f32[256,512]{1,0:T(8,128)} async-done(((f32[2048,512]{1,0:T(8,128)}), f32[256,512]{1,0:T(8,128)}) %reduce-scatter.14.cloned.1.call-update) | async-done | bytes 524304 | tf_op jit(solution)/shard_map/reduce_scatter | solution.py:253
  2485.1 55.1 %reduce-scatter.16.cloned.1.call-done = f32[256,512]{1,0:T(8,128)} async-done(((f32[2048,512]{1,0:T(8,128)}), f32[256,512]{1,0:T(8,128)}) %reduce-scatter.16.cloned.1.call-update) | async-done | bytes 524304 | tf_op jit(solution)/shard_map/reduce_scatter | solution.py:254
  (154 shorter events, 106.3 us)
Async XLA Ops:
  7.2 38.2 %all-gather.16.cloned.1.call-start = ((), (), s32[]{:S(2)}) async-start(), calls=%async_computation.12 | async-start | bytes 3145728 | tf_op jit(solution)/shard_map/all_gather | solution.py:101
  7.9 72.1 %all-gather.14.cloned.1.call-start = ((), (), s32[]{:S(2)}) async-start(), calls=%async_computation.11 | async-start | bytes 3145728 | tf_op jit(solution)/shard_map/all_gather | solution.py:100
  8.7 106.1 %all-gather.10.cloned.1.call-start = ((), (), s32[]{:S(2)}) async-start(), calls=%async_computation.9 | async-start | bytes 3145728 | tf_op jit(solution)/shard_map/all_gather | solution.py:102
  9.4 142.3 %all-gather.18.cloned.1.call-start = ((), (), s32[]{:S(2)}) async-start(), calls=%async_computation.13 | async-start | bytes 5242880 | tf_op jit(solution)/shard_map/all_gather | solution.py:138
  14.9 78.2 %copy-start.24 = (f32[2048]{0:T(1024)}, f32[2048]{0:T(1024)S(1)}, u32[]{:S(2)}) copy-start(f32[2048]{0:T(1024)S(1)} %convert_element_type.133) | copy-start | bytes 24580
  25.4 65.7 %copy-start.11 = (f32[4,256,64]{1,2,0:T(8,128)}, f32[4,256,64]{1,2,0:T(8,128)S(1)}, u32[]{:S(2)}) copy-start(f32[4,256,64]{1,2,0:T(8,128)S(1)} %get-tuple-element.48) | copy-start | bytes 786436
  25.4 65.7 %copy-start.13 = (f32[4,256,64]{1,2,0:T(8,128)}, f32[4,256,64]{1,2,0:T(8,128)S(1)}, u32[]{:S(2)}) copy-start(f32[4,256,64]{1,2,0:T(8,128)S(1)} %get-tuple-element.49) | copy-start | bytes 786436
  91.8 59.9 %copy-start.18 = (bf16[4,256,4,64]{1,3,2,0:T(8,128)(2,1)}, bf16[4,256,4,64]{1,3,2,0:T(8,128)(2,1)S(1)}, u32[]{:S(2)}) copy-start(bf16[4,256,4,64]{1,3,2,0:T(8,128)(2,1)S(1)} %get-tuple-element.40) | copy-start | bytes 1572868
  91.8 59.9 %copy-start.20 = (bf16[4,256,4,64]{1,3,2,0:T(8,128)(2,1)}, bf16[4,256,4,64]{1,3,2,0:T(8,128)(2,1)S(1)}, u32[]{:S(2)}) copy-start(bf16[4,256,4,64]{1,3,2,0:T(8,128)(2,1)S(1)} %get-tuple-element.41) | copy-start | bytes 1572868
  93.0 95.2 %all-gather.12.cloned.1.call-start = ((), (), s32[]{:S(2)}) async-start(), calls=%async_computation.10 | async-start | bytes 5242880 | tf_op jit(solution)/shard_map/all_gather | solution.py:139
  93.1 27.8 %copy-start.26 = (f32[1,2,4,128]{3,1,2,0:T(2,128)}, f32[1,2,4,128]{3,1,2,0:T(2,128)S(1)}, u32[]{:S(2)}) copy-start(f32[1,2,4,128]{3,1,2,0:T(2,128)S(1)} %copy.68) | copy-start | bytes 12292
  98.3 23.2 copy-start.29
  120.9 101.8 %all-gather.20.cloned.1.call-start = ((), (), s32[]{:S(2)}) async-start(), calls=%async_computation.14 | async-start | bytes 3145728 | tf_op jit(solution)/shard_map/all_gather | solution.py:103
  121.5 399.4 %all-reduce.8.cloned.1.call-start = ((), (), s32[]{:S(2)}) async-start(), calls=%async_computation.15 | async-start | bytes 16777216 | tf_op jit(solution)/shard_map/psum | solution.py:148
  127.6 66.8 %copy-start.4 = (pred[4,256,1024]{2,1,0:T(8,128)(4,1)}, pred[4,256,1024]{2,1,0:T(8,128)(4,1)S(1)}, u32[]{:S(2)}) copy-start(pred[4,256,1024]{2,1,0:T(8,128)(4,1)S(1)} %broadcast_compare_fusion) | copy-start | bytes 3145732
  206.1 23.8 copy-start.9
  230.0 395.5 %all-gather.22.cloned.1.call-start = ((), (), s32[]{:S(2)}) async-start(), calls=%async_computation.16 | async-start | bytes 12582912 | tf_op jit(solution)/shard_map/all_gather | solution.py:151
  230.7 500.3 %all-gather.24.cloned.1.call-start = ((), (), s32[]{:S(2)}) async-start(), calls=%async_computation.17 | async-start | bytes 12582912 | tf_op jit(solution)/shard_map/all_gather | solution.py:152
  231.5 605.0 %all-gather.26.cloned.1.call-start = ((), (), s32[]{:S(2)}) async-start(), calls=%async_computation.18 | async-start | bytes 12582912 | tf_op jit(solution)/shard_map/all_gather | solution.py:182
  232.0 1233.3 %all-reduce.12.cloned.1.call-start = ((), (), s32[]{:S(2)}) async-start(), calls=%async_computation.29 | async-start | bytes 33554432 | tf_op jit(solution)/shard_map/psum | solution.py:164
  232.1 655.7 %collective-permute-start = (bf16[2048,1024]{1,0:T(8,128)(2,1)}, bf16[2048,1024]{1,0:T(8,128)(2,1)}, u32[]{:S(2)}, u32[]{:S(2)}) collective-permute-start(bf16[2048,1024]{1,0:T(8,128)(2,1)} %param.24), channel_id=1, source_target_pairs={{0,16},{16,0},{1,17},{17,1},{2,18},{18,2},{3,19},{19,3},{4,20},{20... | collective-permute-start | bytes 12582920 | tf_op jit(solution)/shard_map/ppermute | solution.py:16
  858.3 14.6 copy-start.32
  873.0 14.9 copy-start.7
  902.9 678.4 %reduce-scatter.10.cloned.1.call-start = ((), (), s32[]{:S(2)}) async-start(), calls=%async_computation.19 | async-start | bytes 10485760 | tf_op jit(solution)/shard_map/reduce_scatter | solution.py:226
  1465.3 15.1 copy-start.3
  1465.3 15.1 copy-start.6
  1488.4 6.7 copy-start.5
  1495.1 9.5 copy-start.19
  1504.6 6.3 copy-start.2
  1511.0 144.3 %reduce-scatter.12.cloned.1.call-start = ((), (), s32[]{:S(2)}) async-start(), calls=%async_computation.20 | async-start | bytes 10485760 | tf_op jit(solution)/shard_map/reduce_scatter | solution.py:227
  1533.1 48.2 %copy-start.12 = (f32[4,256,64]{1,2,0:T(8,128)S(1)}, f32[4,256,64]{1,2,0:T(8,128)}, u32[]{:S(2)}) copy-start(f32[4,256,64]{1,2,0:T(8,128)} %copy-done.11) | copy-start | bytes 786436
  1533.1 48.2 %copy-start.14 = (f32[4,256,64]{1,2,0:T(8,128)S(1)}, f32[4,256,64]{1,2,0:T(8,128)}, u32[]{:S(2)}) copy-start(f32[4,256,64]{1,2,0:T(8,128)} %copy-done.13) | copy-start | bytes 786436
  1533.1 427.6 %all-reduce.10.cloned.1.call-start = ((), (), s32[]{:S(2)}) async-start(), calls=%async_computation.21 | async-start | bytes 16777216 | tf_op jit(solution)/shard_map/psum | solution.py:240
  1585.0 76.4 %copy-start.16 = (bf16[2048,512]{1,0:T(8,128)(2,1)S(1)}, bf16[2048,512]{1,0:T(8,128)(2,1)}, u32[]{:S(2)}) copy-start(bf16[2048,512]{1,0:T(8,128)(2,1)} %all-gather.14.cloned.1.call-done) | copy-start | bytes 6291460
  1655.3 6.1 copy-start.22
  1669.7 344.9 %reduce-scatter.20.cloned.1.call-start = ((), (), s32[]{:S(2)}) async-start(), calls=%async_computation.25 | async-start | bytes 4718592 | tf_op jit(solution)/shard_map/reduce_scatter | solution.py:256
  1678.7 456.1 %reduce-scatter.22.cloned.1.call-start = ((), (), s32[]{:S(2)}) async-start(), calls=%async_computation.26 | async-start | bytes 18874368 | tf_op jit(solution)/shard_map/reduce_scatter | solution.py:258
  1694.1 560.8 %reduce-scatter.24.cloned.1.call-start = ((), (), s32[]{:S(2)}) async-start(), calls=%async_computation.27 | async-start | bytes 18874368 | tf_op jit(solution)/shard_map/reduce_scatter | solution.py:259
  1709.4 665.6 %reduce-scatter.26.cloned.1.call-start = ((), (), s32[]{:S(2)}) async-start(), calls=%async_computation.28 | async-start | bytes 18874368 | tf_op jit(solution)/shard_map/reduce_scatter | solution.py:260
  1725.0 6.8 copy-start.23
  1725.0 705.1 %reduce-scatter.18.cloned.1.call-start = ((), (), s32[]{:S(2)}) async-start(), calls=%async_computation.24 | async-start | bytes 4718592 | tf_op jit(solution)/shard_map/reduce_scatter | solution.py:255
  1731.7 753.4 %reduce-scatter.14.cloned.1.call-start = ((), (), s32[]{:S(2)}) async-start(), calls=%async_computation.22 | async-start | bytes 4718592 | tf_op jit(solution)/shard_map/reduce_scatter | solution.py:253
  1731.8 6.7 copy-start.21
  1738.4 6.7 copy-start.31
  1738.4 7.9 copy-start.27
  1738.4 222.2 %copy-start.25 = (f32[2048]{0:T(1024)S(1)}, f32[2048]{0:T(1024)}, u32[]{:S(2)}) copy-start(f32[2048]{0:T(1024)} %copy-done.24) | copy-start | bytes 24580
  1738.4 801.8 %reduce-scatter.16.cloned.1.call-start = ((), (), s32[]{:S(2)}) async-start(), calls=%async_computation.23 | async-start | bytes 4718592 | tf_op jit(solution)/shard_map/reduce_scatter | solution.py:254
  1745.0 222.0 %copy-start.28 = (f32[2048]{0:T(1024)S(1)}, f32[2048]{0:T(1024)}, u32[]{:S(2)}) copy-start(f32[2048]{0:T(1024)} %get-tuple-element.21) | copy-start | bytes 24580
  (7 other events, 23.2 us)
Sparse Core Ops, SparseCore 0:
  9.5 35.8 all-gather.15
  46.9 33.0 all-gather.13
  81.6 33.0 all-gather.9
  116.7 34.9 all-gather.17
  153.7 34.4 all-gather.11
  189.6 33.0 all-gather.19
  230.1 290.8 all-reduce.7
  522.5 102.9 all-gather.21
  627.0 103.9 all-gather.23
  732.4 103.9 all-gather.25
  903.0 562.2 all-reduce.11
  1511.1 70.1 reduce-scatter.9
  1583.8 71.3 reduce-scatter.11
  1669.8 290.8 all-reduce.9
  1964.5 50.0 reduce-scatter.19
  2018.6 116.1 reduce-scatter.21
  2138.8 116.1 reduce-scatter.23
  2259.0 115.9 reduce-scatter.25
  2378.9 51.1 reduce-scatter.17
  2433.9 51.1 reduce-scatter.13
  2489.1 51.1 reduce-scatter.15
